TPU v7x, 32 devices: a whole 2x2x4 slice. The times are simulated.
32 devices in a mesh: dp: 8 (over z, y), fsdp: 4 (over x, core).
Axes of the slice: x: 2, y: 2, z: 4, core: 2. Of those that a mesh axis runs over, the one named last changes fastest.
Arguments:
- tokens: bfloat16 [16384, 4096], P(('dp', 'fsdp')), may hold values from -0.75 to 0.75
- doc_ids: int32 [16384], P(('dp', 'fsdp')), may hold values from 0 to 15, never falling along the last dimension, each value on 1 to 2048 neighbouring positions
- attn_gain: float32 [4096], replicated, may hold values from 0.1 to 1.9
- mlp_gain: float32 [4096], replicated, may hold values from 0.1 to 1.9
- w_query: bfloat16 [4096, 512], P(('dp', 'fsdp')), may hold values from -1 to 1
- w_key_value: bfloat16 [4096, 256], P(('dp', 'fsdp')), may hold values from -3 to 3
- w_out: bfloat16 [512, 4096], P(None, ('dp', 'fsdp')), may hold values from -0.25 to 0.25
- w_gate: bfloat16 [4096, 1024], P(('dp', 'fsdp')), may hold values from -0.09375 to 0.09375
- w_up: bfloat16 [4096, 1024], P(('dp', 'fsdp')), may hold values from -0.09375 to 0.09375
- w_down: bfloat16 [1024, 4096], P(None, ('dp', 'fsdp')), may hold values from -0.1875 to 0.1875
Outputs:
- mixed: bfloat16 [16384, 4096], P(('dp', 'fsdp'))
Inputs may be any that keep to these rules, and one draw needn't show every extreme that they name: `doc_ids`: document numbers never fall along the pack, and every document has at most 2048 tokens.
All inputs are finite; a program needn't handle non-finite values.
Results may differ from a plain program's by a relative error of at most 0.02.
The roundings to bfloat16 on the way count: a program that leaves them out, or rounds other values in their place, can miss the bound.
Values may be sent and summed in bfloat16 or wider, within the bound.
A program may use at most 128 MiB of HBM per device.

v0:
```python
import math

import jax
import jax.numpy as jnp
from jax import lax
from jax.sharding import PartitionSpec as P

SPAN = 4


EPS = 1e-05
THETA = 500000.0
NEGATIVE = -1e30


def shifted(array, axis, by):
    length = lax.axis_size(axis)
    pairs = [(i, i + by) for i in range(length) if 0 <= i + by < length]
    return lax.ppermute(array, axis, pairs)


def rms_scale(values, gain):
    wide = values.astype(jnp.float32)
    power = jnp.mean(wide * wide, axis=-1, keepdims=True)
    return (wide * lax.rsqrt(power + EPS) * gain).astype(jnp.bfloat16)


def rotate(values, position):
    head = values.shape[-1]
    half = head // 2
    freqs = THETA ** (-2.0 * jnp.arange(half, dtype=jnp.float32) / head)
    angle = position.astype(jnp.float32)[:, None, None] * freqs[None, None, :]
    cosine = jnp.cos(angle)
    sine = jnp.sin(angle)
    first = values[..., :half]
    second = values[..., half:]
    return jnp.concatenate(
        [first * cosine - second * sine, second * cosine + first * sine], axis=-1
    )


def head_scores(query, keys):
    return jnp.einsum("qhd,kd->hqk", query, keys, preferred_element_type=jnp.float32) / math.sqrt(
        query.shape[-1]
    )


def weigh_values(weights, values):
    return jnp.einsum(
        "hqk,kd->qhd", weights.astype(jnp.bfloat16), values, preferred_element_type=jnp.float32
    )


def attend_dense(query, keys, values, key_marks, marks, offset):
    scores = head_scores(query, keys)
    key_index = jnp.arange(keys.shape[0], dtype=jnp.int32)
    query_index = jnp.arange(query.shape[0], dtype=jnp.int32) + offset
    allowed = (key_marks[None, :] == marks[:, None]) & (key_index[None, :] <= query_index[:, None])
    scores = jnp.where(allowed[None, :, :], scores, NEGATIVE)
    peak = jnp.max(scores, axis=2, keepdims=True)
    weights = jnp.exp(scores - peak)
    totals = jnp.sum(weights, axis=2)
    return weigh_values(weights, values) / jnp.transpose(totals)[:, :, None]


def per_device(
    tokens, doc_ids, attn_gain, mlp_gain, w_query, w_key_value, w_out, w_gate, w_up, w_down
):
    rows = tokens.shape[0]
    rank = lax.axis_index(("dp", "fsdp"))
    normed = rms_scale(tokens, attn_gain)
    query_width = w_query.shape[1]
    pair_width = w_key_value.shape[1]
    head = pair_width // 2
    heads = query_width // head
    group_query, group_pair = (
        lax.all_gather(w_query, "fsdp", axis=0, tiled=True),
        lax.all_gather(w_key_value, "fsdp", axis=0, tiled=True),
    )
    pieces = (
        lax.all_gather(group_query, "dp", axis=0, tiled=True),
        lax.all_gather(group_pair, "dp", axis=0, tiled=True),
    )
    columns = normed
    query_raw = jnp.dot(columns, pieces[0], preferred_element_type=jnp.float32)
    pair_raw = jnp.dot(columns, pieces[1], preferred_element_type=jnp.float32)
    position = rank * rows + jnp.arange(rows, dtype=jnp.int32)
    query = rotate(query_raw.reshape(rows, heads, head), position).astype(jnp.bfloat16)
    keys = rotate(pair_raw[:, None, :head], position)[:, 0, :].astype(jnp.bfloat16)
    values = pair_raw[:, head:].astype(jnp.bfloat16)
    own_pairs = jnp.concatenate([keys, values], axis=1)
    marks = doc_ids + 1
    amounts = [1] + [1 << level for level in range(SPAN.bit_length() - 1)]
    held_pairs = own_pairs
    held_marks = marks
    for order, amount in enumerate(amounts):
        moved_pairs, moved_marks = shifted((held_pairs, held_marks), ("dp", "fsdp"), amount)
        if order == 0:
            held_pairs = moved_pairs
            held_marks = moved_marks
        else:
            held_pairs = jnp.concatenate([moved_pairs, held_pairs], axis=0)
            held_marks = jnp.concatenate([moved_marks, held_marks], axis=0)
    every_pair = jnp.concatenate([held_pairs, own_pairs], axis=0)
    every_mark = jnp.concatenate([held_marks, marks], axis=0)
    mixed = attend_dense(
        query, every_pair[:, :head], every_pair[:, head:], every_mark, marks, held_pairs.shape[0]
    )
    attended = mixed.reshape(rows, query_width).astype(jnp.bfloat16)
    projected = jnp.dot(
        attended,
        lax.all_gather(w_out, ("dp", "fsdp"), axis=1, tiled=True),
        preferred_element_type=jnp.float32,
    )
    resid = (tokens.astype(jnp.float32) + projected).astype(jnp.bfloat16)
    resid = lax.optimization_barrier(resid)
    normed_mlp = rms_scale(resid, mlp_gain)
    pieces = (
        lax.all_gather(w_gate, ("dp", "fsdp"), axis=0, tiled=True),
        lax.all_gather(w_up, ("dp", "fsdp"), axis=0, tiled=True),
    )
    columns = normed_mlp
    gate = jnp.dot(columns, pieces[0], preferred_element_type=jnp.float32)
    up_value = jnp.dot(columns, pieces[1], preferred_element_type=jnp.float32)
    hidden = (jax.nn.silu(gate) * up_value).astype(jnp.bfloat16)
    down = jnp.dot(
        hidden,
        lax.all_gather(w_down, ("dp", "fsdp"), axis=1, tiled=True),
        preferred_element_type=jnp.float32,
    )
    return (resid.astype(jnp.float32) + down).astype(jnp.bfloat16)


def solution(mesh):
    in_specs = (
        P(("dp", "fsdp"), None),
        P(("dp", "fsdp")),
        P(),
        P(),
        P(("dp", "fsdp"), None),
        P(("dp", "fsdp"), None),
        P(None, ("dp", "fsdp")),
        P(("dp", "fsdp"), None),
        P(("dp", "fsdp"), None),
        P(None, ("dp", "fsdp")),
    )
    out_specs = P(("dp", "fsdp"), None)
    return jax.shard_map(
        per_device, mesh=mesh, in_specs=in_specs, out_specs=out_specs, check_vma=False
    )
```

profile of v0, /device:TPU:11, one launch (start us, length us, event | category | flops | bytes accessed | tf_op | source)
XLA Modules:
  0.0 479.2 jit_solution(8188637932389461897)
XLA Ops:
  6.5 7.1 %all_gather.24 = bf16[512,256]{1,0:T(8,128)(2,1)} all-gather(bf16[128,256]{1,0:T(8,128)(2,1)} %param.15), channel_id=1, replica_groups=mesh['dp'=8,'fsdp'=4] {'fsdp'}, dimensions={0}, use_global_device_ids=true | all-gather | bytes 327680 | tf_op jit(solution)/shard_map/all_gather | solution.py:78
  13.7 9.2 %all_gather.26 = bf16[512,512]{1,0:T(8,128)(2,1)} all-gather(bf16[128,512]{1,0:T(8,128)(2,1)} %param.14), channel_id=1, replica_groups=mesh['dp'=8,'fsdp'=4] {'fsdp'}, dimensions={0}, use_global_device_ids=true | all-gather | bytes 655360 | tf_op jit(solution)/shard_map/all_gather | solution.py:77
  25.4 3.1 fusion.6
  28.5 33.9 %all-gather.7.cloned.1.call-done = bf16[4096,256]{1,0:T(8,128)(2,1)} async-done(((bf16[512,256]{1,0:T(8,128)(2,1)}), bf16[4096,256]{1,0:T(8,128)(2,1)}) %all-gather.7.cloned.1.call-update) | async-done | bytes 2097168 | tf_op jit(solution)/shard_map/all_gather | solution.py:82
  62.5 4.4 fusion.23
  67.6 3.8 collective-permute-start
  74.8 5.3 %collective-permute-start.4 = (s32[512]{0:T(512)S(1)}, s32[512]{0:T(512)S(1)}, u32[]{:S(2)}, u32[]{:S(2)}) collective-permute-start(s32[512]{0:T(512)S(1)} %collective-permute-done.3), channel_id=1, source_target_pairs={{0,1},{1,2},{2,3},{3,4},{4,5},{5,6},{6,7},{7,8},{8,9},{9,10},{10,1... | collective-permute-start | bytes 6152 | tf_op jit(solution)/shard_map/ppermute | solution.py:19
  83.1 6.1 %collective-permute-start.5 = (s32[1024]{0:T(1024)S(1)}, s32[1024]{0:T(1024)S(1)}, u32[]{:S(2)}, u32[]{:S(2)}) collective-permute-start(s32[1024]{0:T(1024)S(1)} %pad_add_fusion.1), channel_id=1, source_target_pairs={{0,2},{1,3},{2,4},{3,5},{4,6},{5,7},{6,8},{7,9},{8,10},{9,11},{10,... | collective-permute-start | bytes 12296 | tf_op jit(solution)/shard_map/ppermute | solution.py:19
  90.0 7.0 %collective-permute-start.2 = (bf16[1024,256]{0,1:T(8,128)(2,1)S(1)}, bf16[1024,256]{0,1:T(8,128)(2,1)S(1)}, u32[]{:S(2)}, u32[]{:S(2)}) collective-permute-start(bf16[1024,256]{0,1:T(8,128)(2,1)S(1)} %pad_maximum_fusion), channel_id=1, source_target_pairs={{0,2},{1,3},{2,4},{3,5},{4,6},{5,7},{6,8},{7,9},{8,10},{9,11},{10,... | collective-permute-start | bytes 1572872 | tf_op jit(solution)/shard_map/ppermute | solution.py:19
  98.4 14.0 %collective-permute-done.2 = bf16[1024,256]{0,1:T(8,128)(2,1)S(1)} collective-permute-done((bf16[1024,256]{0,1:T(8,128)(2,1)S(1)}, bf16[1024,256]{0,1:T(8,128)(2,1)S(1)}, u32[]{:S(2)}, u32[]{:S(2)}) %collective-permute-start.2) | collective-permute-done | bytes 524320 | tf_op jit(solution)/shard_map/ppermute | solution.py:19
  113.6 23.3 %all-gather.9.cloned.1.call-done = bf16[4096,512]{1,0:T(8,128)(2,1)} async-done(((bf16[512,512]{1,0:T(8,128)(2,1)}), bf16[4096,512]{1,0:T(8,128)(2,1)}) %all-gather.9.cloned.1.call-update) | async-done | bytes 4194320 | tf_op jit(solution)/shard_map/all_gather | solution.py:81
  136.9 5.9 %fusion.21 = f32[512,512]{0,1:T(8,128)S(1)} fusion(bf16[4096,512]{1,0:T(8,128)(2,1)} %all-gather.9.cloned.1.call-done, bf16[512,4096]{1,0:T(8,128)(2,1)} %param.10, f32[4096]{0:T(1024)S(1)} %copy-done.3, f32[512]{0:T(512)S(1)} %add_rsqrt_fusion.1), kind=kOutput, calls=%fused_computation.27 | convolution fusion | flops 2155872256 | bytes 9455616 | tf_op jit(solution)/shard_map/dot_general | solution.py:85
  148.0 5.3 %fusion.2 = (f32[4,512]{1,0:T(4,128)S(1)}, f32[2560,512,4]{1,0,2:T(8,128)S(1)}) fusion(pred[512,2560]{0,1:T(8,128)(4,1)S(1)} %fusion.14, bf16[512,4,64]{2,0,1:T(8,128)(2,1)S(1)} %get-tuple-element.6, bf16[512,4,64]{2,0,1:T(8,128)(2,1)S(1)} %get-tuple-element.5, bf16[2560,256]{0,1:T(8,128)(2,1)} %maximum_maximum_fusion), kind=kOutput, calls=%fused_computation.4 | convolution fusion | flops 1358952448 | bytes 23470080 | tf_op jit(solution)/shard_map/qhd,kd->hqk/dot_general | solution.py:43
  153.3 4.5 fusion
  157.9 6.1 %divide_convert_fusion = bf16[512,4,128]{0,2,1:T(8,128)(2,1)S(1)} fusion(f32[2560,512,4]{1,0,2:T(8,128)S(1)} %get-tuple-element.14, f32[4,512]{1,0:T(4,128)S(1)} %get-tuple-element.13, pred[512,2560]{0,1:T(8,128)(4,1)S(1)} %fusion.14, bf16[2560,256]{0,1:T(8,128)(2,1)S(1)} %copy-done.1, f32[512,4]{0,1:T(4,128)S(1)} %bitcast.42), kind=kOutput, calls=%fused_computation.29 | convolution fusion | flops 1363673088 | bytes 23478272 | tf_op jit(solution)/shard_map/hqk,kd->qhd/dot_general | solution.py:49
  164.0 48.9 %all-gather.11.cloned.1.call-done = bf16[512,4096]{1,0:T(8,128)(2,1)} async-done(((bf16[512,128]{1,0:T(8,128)(2,1)}), bf16[512,4096]{1,0:T(8,128)(2,1)}) %all-gather.11.cloned.1.call-update) | async-done | bytes 4194320 | tf_op jit(solution)/shard_map/all_gather | solution.py:112
  212.9 5.9 %fusion.9 = bf16[512,4096]{1,0:T(8,128)(2,1)S(1)} fusion(bf16[512,4096]{1,0:T(8,128)(2,1)} %param.10, bf16[512,512]{0,1:T(8,128)(2,1)S(1)} %bitcast.41, bf16[512,4096]{1,0:T(8,128)(2,1)} %all-gather.11.cloned.1.call-done), kind=kOutput, calls=%fused_computation.16 | convolution fusion | flops 2153775104 | bytes 13107200 | tf_op jit(solution)/shard_map/dot_general | solution.py:110
  218.8 2.0 copy-done
  221.7 71.8 %all-gather.13.cloned.1.call-done = bf16[4096,1024]{1,0:T(8,128)(2,1)} async-done(((bf16[128,1024]{1,0:T(8,128)(2,1)}), bf16[4096,1024]{1,0:T(8,128)(2,1)}) %all-gather.13.cloned.1.call-update) | async-done | bytes 8388624 | tf_op jit(solution)/shard_map/all_gather | solution.py:119
  293.5 8.3 %fusion.19 = f32[512,1024]{1,0:T(8,128)S(1)} fusion(bf16[4096,1024]{1,0:T(8,128)(2,1)} %all-gather.13.cloned.1.call-done, bf16[512,4096]{1,0:T(8,128)(2,1)} %copy-done, f32[4096]{0:T(1024)S(1)} %copy-done.4, f32[512]{0:T(512)S(1)} %add_rsqrt_fusion), kind=kOutput, calls=%fused_computation.26 | convolution fusion | flops 4303355904 | bytes 14698496 | tf_op jit(solution)/shard_map/dot_general | solution.py:123
  301.7 70.1 %all-gather.15.cloned.1.call-done = bf16[4096,1024]{1,0:T(8,128)(2,1)} async-done(((bf16[128,1024]{1,0:T(8,128)(2,1)}), bf16[4096,1024]{1,0:T(8,128)(2,1)}) %all-gather.15.cloned.1.call-update) | async-done | bytes 8388624 | tf_op jit(solution)/shard_map/all_gather | solution.py:120
  371.9 9.4 %multiply_convert_fusion = bf16[512,1024]{1,0:T(8,128)(2,1)S(1)} fusion(f32[512,1024]{1,0:T(8,128)S(1)} %fusion.19, bf16[4096,1024]{1,0:T(8,128)(2,1)} %all-gather.15.cloned.1.call-done, bf16[512,4096]{1,0:T(8,128)(2,1)} %copy-done, f32[4096]{0:T(1024)S(1)} %copy-done.4, f32[512]{0:T(512)S(1)} %add_rsqrt_fusion), kind=kOutput, calls=%fused_computation.23 | convolution fusion | flops 4306501632 | bytes 15747072 | tf_op jit(solution)/shard_map/dot_general | solution.py:124
  381.2 81.0 %all-gather.17.cloned.1.call-done = bf16[1024,4096]{1,0:T(8,128)(2,1)} async-done(((bf16[1024,128]{1,0:T(8,128)(2,1)}), bf16[1024,4096]{1,0:T(8,128)(2,1)}) %all-gather.17.cloned.1.call-update) | async-done | bytes 8388624 | tf_op jit(solution)/shard_map/all_gather | solution.py:128
  462.3 10.1 %fusion.13 = bf16[512,4096]{1,0:T(8,128)(2,1)} fusion(bf16[512,4096]{1,0:T(8,128)(2,1)} %copy-done, bf16[512,1024]{1,0:T(8,128)(2,1)S(1)} %multiply_convert_fusion, bf16[1024,4096]{1,0:T(8,128)(2,1)} %all-gather.17.cloned.1.call-done), kind=kOutput, calls=%fused_computation.20 | convolution fusion | flops 4301258752 | bytes 17825792 | tf_op jit(solution)/shard_map/dot_general | solution.py:126
  (50 shorter events, 18.9 us)
Async XLA Ops:
  6.5 55.9 %copy-start.3 = (f32[4096]{0:T(1024)S(1)}, f32[4096]{0:T(1024)}, u32[]{:S(2)}) copy-start(f32[4096]{0:T(1024)} %param.12) | copy-start | bytes 49156
  6.5 55.9 %all-gather.7.cloned.1.call-start = ((), (), s32[]{:S(2)}) async-start(), calls=%async_computation | async-start | bytes 2359296 | tf_op jit(solution)/shard_map/all_gather | solution.py:82
  13.6 123.2 %all-gather.9.cloned.1.call-start = ((), (), s32[]{:S(2)}) async-start(), calls=%async_computation.1 | async-start | bytes 4718592 | tf_op jit(solution)/shard_map/all_gather | solution.py:81
  22.9 190.0 %all-gather.11.cloned.1.call-start = ((), (), s32[]{:S(2)}) async-start(), calls=%async_computation.2 | async-start | bytes 4325376 | tf_op jit(solution)/shard_map/all_gather | solution.py:112
  23.7 269.8 %all-gather.13.cloned.1.call-start = ((), (), s32[]{:S(2)}) async-start(), calls=%async_computation.3 | async-start | bytes 8650752 | tf_op jit(solution)/shard_map/all_gather | solution.py:119
  24.2 347.6 %all-gather.15.cloned.1.call-start = ((), (), s32[]{:S(2)}) async-start(), calls=%async_computation.4 | async-start | bytes 8650752 | tf_op jit(solution)/shard_map/all_gather | solution.py:120
  24.8 437.4 %all-gather.17.cloned.1.call-start = ((), (), s32[]{:S(2)}) async-start(), calls=%async_computation.5 | async-start | bytes 8650752 | tf_op jit(solution)/shard_map/all_gather | solution.py:128
  28.5 42.9 %copy-start.2 = (s32[512]{0:T(512)S(1)}, s32[512]{0:T(512)}, u32[]{:S(2)}) copy-start(s32[512]{0:T(512)} %param.11) | copy-start | bytes 6148
  67.6 13.5 %collective-permute-start = (bf16[512,256]{0,1:T(8,128)(2,1)S(1)}, bf16[512,256]{0,1:T(8,128)(2,1)S(1)}, u32[]{:S(2)}, u32[]{:S(2)}) collective-permute-start(bf16[512,256]{0,1:T(8,128)(2,1)S(1)} %pad_maximum_fusion.1), channel_id=1, source_target_pairs={{0,1},{1,2},{2,3},{3,4},{4,5},{5,6},{6,7},{7,8},{8,9},{9,10},{10,1... | collective-permute-start | bytes 786440 | tf_op jit(solution)/shard_map/ppermute | solution.py:19
  71.4 3.3 collective-permute-start.3
  74.8 8.3 %collective-permute-start.4 = (s32[512]{0:T(512)S(1)}, s32[512]{0:T(512)S(1)}, u32[]{:S(2)}, u32[]{:S(2)}) collective-permute-start(s32[512]{0:T(512)S(1)} %collective-permute-done.3), channel_id=1, source_target_pairs={{0,1},{1,2},{2,3},{3,4},{4,5},{5,6},{6,7},{7,8},{8,9},{9,10},{10,1... | collective-permute-start | bytes 6152 | tf_op jit(solution)/shard_map/ppermute | solution.py:19
  81.1 8.8 %collective-permute-start.1 = (bf16[512,256]{0,1:T(8,128)(2,1)S(1)}, bf16[512,256]{0,1:T(8,128)(2,1)S(1)}, u32[]{:S(2)}, u32[]{:S(2)}) collective-permute-start(bf16[512,256]{0,1:T(8,128)(2,1)S(1)} %collective-permute-done), channel_id=1, source_target_pairs={{0,1},{1,2},{2,3},{3,4},{4,5},{5,6},{6,7},{7,8},{8,9},{9,10},{10,1... | collective-permute-start | bytes 786440 | tf_op jit(solution)/shard_map/ppermute | solution.py:19
  83.1 6.8 %collective-permute-start.5 = (s32[1024]{0:T(1024)S(1)}, s32[1024]{0:T(1024)S(1)}, u32[]{:S(2)}, u32[]{:S(2)}) collective-permute-start(s32[1024]{0:T(1024)S(1)} %pad_add_fusion.1), channel_id=1, source_target_pairs={{0,2},{1,3},{2,4},{3,5},{4,6},{5,7},{6,8},{7,9},{8,10},{9,11},{10,... | collective-permute-start | bytes 12296 | tf_op jit(solution)/shard_map/ppermute | solution.py:19
  90.0 22.5 %collective-permute-start.2 = (bf16[1024,256]{0,1:T(8,128)(2,1)S(1)}, bf16[1024,256]{0,1:T(8,128)(2,1)S(1)}, u32[]{:S(2)}, u32[]{:S(2)}) collective-permute-start(bf16[1024,256]{0,1:T(8,128)(2,1)S(1)} %pad_maximum_fusion), channel_id=1, source_target_pairs={{0,2},{1,3},{2,4},{3,5},{4,6},{5,7},{6,8},{7,9},{8,10},{9,11},{10,... | collective-permute-start | bytes 1572872 | tf_op jit(solution)/shard_map/ppermute | solution.py:19
  153.3 4.6 copy-start.1
  218.7 2.0 copy-start
  220.8 72.7 %copy-start.4 = (f32[4096]{0:T(1024)S(1)}, f32[4096]{0:T(1024)}, u32[]{:S(2)}) copy-start(f32[4096]{0:T(1024)} %param.13) | copy-start | bytes 49156
Sparse Core Ops, SparseCore 0:
  13.7 48.6 all-gather.6
  64.6 72.2 all-gather.8
  139.7 73.1 all-gather.10
  215.6 77.8 all-gather.12
  296.2 75.6 all-gather.14
  374.6 87.6 all-gather.16
where the time goes:
time: 484 us; the launch traced here: 479 us
  waiting for transfers between devices  347 us (72%)
  matrix products  55.3 us (11%)
  starting transfers between devices  26.3 us (5%)
  blocking collectives  16.3 us (3%)
  other arithmetic  14.3 us (3%)
  between operations  13.8 us (3%)
  local copies, waits for them, and re-layouts  5.75 us (1%)
    all_gather x1, waiting for transfers between devices, per_device(): lax.all_gather(w_down, ('dp', 'fsdp'), axis=1, tiled=True)  81 us
    all_gather x1, waiting for transfers between devices, per_device(): lax.all_gather(w_gate, ('dp', 'fsdp'), axis=0, tiled=True)  71.8 us
    all_gather x1, waiting for transfers between devices, per_device(): lax.all_gather(w_up, ('dp', 'fsdp'), axis=0, tiled=True)  70.1 us
    all_gather x1, waiting for transfers between devices, per_device(): lax.all_gather(w_out, ('dp', 'fsdp'), axis=1, tiled=True)  48.9 us
    all_gather x1, waiting for transfers between devices, per_device(): lax.all_gather(group_pair, 'dp', axis=0, tiled=True)  33.9 us
    ppermute x6, starting transfers between devices, shifted(): return lax.ppermute(array, axis, pairs)  26.1 us
    all_gather x1, waiting for transfers between devices, per_device(): lax.all_gather(group_query, 'dp', axis=0, tiled=True)  23.3 us
    ppermute x6, waiting for transfers between devices, shifted(): return lax.ppermute(array, axis, pairs)  16.2 us
  transfers between devices with their start and end apart: 12, of which 9 were waited for; matrix products, arithmetic and copies ran while one was open for 13% of the time, Pallas kernels for 0%

commit v1 on v0

--- a/solution.py
+++ b/solution.py
@@ -1,8 +1,11 @@
+import functools
 import math
 
 import jax
 import jax.numpy as jnp
 from jax import lax
+from jax.experimental import pallas as pl
+from jax.experimental.pallas import tpu as pltpu
 from jax.sharding import PartitionSpec as P
 
 SPAN = 4
@@ -63,6 +66,184 @@
     return weigh_values(weights, values) / jnp.transpose(totals)[:, :, None]
 
 
+MESH = pl.DeviceIdType.MESH
+
+
+class Gather:
+    def __init__(self, spot, own, full, send, recv, local, row):
+        self.own, self.full = own, full
+        self.send, self.recv, self.local, self.row = send, recv, local, row
+        self.dp, self.fsdp, self.depth = spot
+        self.z, self.y = self.dp // 2, self.dp % 2
+        self.x, self.c = self.fsdp // 2, self.fsdp % 2
+        self.right = (self.dp, (1 - self.x) * 2 + self.c)
+        self.up = (self.z * 2 + 1 - self.y, self.fsdp)
+        self.twin = (self.dp, self.x * 2 + 1 - self.c)
+        self.base = self.depth - 1
+
+    def peers(self):
+        others = [
+            (lax.rem(self.z + step, self.depth) * 2 + self.y, self.fsdp)
+            for step in range(1, self.depth)
+        ]
+        return others + [self.right, self.up, self.twin]
+
+    def copy(self, number, source, target, device):
+        return pltpu.make_async_remote_copy(
+            src_ref=source,
+            dst_ref=target,
+            send_sem=self.send.at[self.row, number],
+            recv_sem=self.recv.at[self.row, number],
+            device_id=device,
+            device_id_type=MESH,
+        )
+
+    def column(self, y, x, number, device, c=None):
+        c = self.c if c is None else c
+        part = self.full.at[:, y, x, c]
+        return self.copy(number, part, part, device)
+
+    def half(self, y, x, which, number, device):
+        middle = self.depth // 2
+        part = self.full.at[pl.ds(which * middle, middle), y, x, self.c]
+        return self.copy(number, part, part, device)
+
+    def mine(self):
+        return pltpu.make_async_copy(
+            self.own, self.full.at[self.z, self.y, self.x, self.c], self.local.at[self.row]
+        )
+
+    def along(self, step):
+        there = (lax.rem(self.z + step, self.depth) * 2 + self.y, self.fsdp)
+        return self.copy(
+            step - 1, self.own, self.full.at[self.z, self.y, self.x, self.c], there
+        )
+
+    def s0(self):
+        self.mine().start()
+        for step in range(1, self.depth):
+            self.along(step).start()
+
+    def s1(self):
+        self.mine().wait()
+        for step in range(1, self.depth):
+            self.along(step).wait_recv()
+        self.column(self.y, self.x, self.base, self.right).start()
+        self.column(self.y, self.x, self.base + 1, self.up).start()
+        self.column(self.y, self.x, self.base + 4, self.twin).start()
+
+    def s2(self):
+        self.column(self.y, self.x, self.base, self.right).wait_recv()
+        self.column(self.y, self.x, self.base + 1, self.up).wait_recv()
+        self.half(1 - self.y, self.x, 0, self.base + 2, self.right).start()
+        self.half(self.y, 1 - self.x, 1, self.base + 3, self.up).start()
+        self.column(self.y, 1 - self.x, self.base + 5, self.twin).start()
+        self.column(1 - self.y, self.x, self.base + 6, self.twin).start()
+
+    def s3(self):
+        self.half(1 - self.y, self.x, 0, self.base + 2, self.right).wait_recv()
+        self.half(self.y, 1 - self.x, 1, self.base + 3, self.up).wait_recv()
+        self.column(1 - self.y, 1 - self.x, self.base + 7, self.twin).start()
+
+    def s4(self):
+        for step in range(1, self.depth):
+            self.along(step).wait_send()
+        self.column(self.y, self.x, self.base, self.right).wait_send()
+        self.column(self.y, self.x, self.base + 1, self.up).wait_send()
+        self.half(1 - self.y, self.x, 0, self.base + 2, self.right).wait_send()
+        self.half(self.y, 1 - self.x, 1, self.base + 3, self.up).wait_send()
+        self.column(self.y, self.x, self.base + 4, self.twin).wait()
+        self.column(self.y, 1 - self.x, self.base + 5, self.twin).wait()
+        self.column(1 - self.y, self.x, self.base + 6, self.twin).wait()
+        self.column(1 - self.y, 1 - self.x, self.base + 7, self.twin).wait()
+
+
+def greet(peers):
+    barrier = pltpu.get_barrier_semaphore()
+    for device in peers:
+        pl.semaphore_signal(barrier, inc=1, device_id=device, device_id_type=MESH)
+    pl.semaphore_wait(barrier, len(peers))
+
+
+def gather_kernel(depth, count, *refs):
+    owns, fulls = refs[:count], refs[count : 2 * count]
+    send, recv, local = refs[2 * count :]
+    spot = (lax.axis_index("dp"), lax.axis_index("fsdp"), depth)
+    rides = [Gather(spot, owns[i], fulls[i], send, recv, local, i) for i in range(count)]
+    greet(rides[0].peers())
+    for ride in rides:
+        ride.s0()
+    for slot in range(count + 3):
+        for stage, lag in (("s1", 0), ("s2", 1), ("s3", 2), ("s4", 3)):
+            if 0 <= slot - lag < count:
+                getattr(rides[slot - lag], stage)()
+
+
+def gather_all(arrays):
+    depth = lax.axis_size("dp") // 2
+    count = len(arrays)
+    copies = depth - 1 + 8
+    return pl.pallas_call(
+        functools.partial(gather_kernel, depth, count),
+        out_shape=[
+            jax.ShapeDtypeStruct((depth, 2, 2, 2) + array.shape, array.dtype) for array in arrays
+        ],
+        in_specs=[pl.BlockSpec(memory_space=pl.ANY)] * count,
+        out_specs=[pl.BlockSpec(memory_space=pl.ANY)] * count,
+        scratch_shapes=[
+            pltpu.SemaphoreType.DMA((count, copies)),
+            pltpu.SemaphoreType.DMA((count, copies)),
+            pltpu.SemaphoreType.DMA((count,)),
+        ],
+        compiler_params=pltpu.CompilerParams(
+            collective_id=0, has_side_effects=True, vmem_limit_bytes=4 << 20
+        ),
+    )(*arrays)
+
+
+def by_rows(full):
+    return full.reshape(-1, full.shape[-1])
+
+
+def by_columns(full):
+    blocks = full.reshape((-1,) + full.shape[-2:])
+    return jnp.transpose(blocks, (1, 0, 2)).reshape(blocks.shape[1], -1)
+
+
+def gather_plain(w_query, w_key_value, w_out, w_gate, w_up, w_down):
+    both = ("dp", "fsdp")
+    return (
+        jnp.concatenate(
+            [
+                lax.all_gather(w_query, both, axis=0, tiled=True),
+                lax.all_gather(w_key_value, both, axis=0, tiled=True),
+            ],
+            axis=1,
+        ),
+        lax.all_gather(w_out, both, axis=1, tiled=True),
+        lax.all_gather(w_gate, both, axis=0, tiled=True),
+        lax.all_gather(w_up, both, axis=0, tiled=True),
+        lax.all_gather(w_down, both, axis=1, tiled=True),
+    )
+
+
+def aligned(w_out):
+    lanes = 128
+    return (
+        w_out.shape[1] % lanes == 0
+        and lax.axis_size("fsdp") == 4
+        and lax.axis_size("dp") % 4 == 0
+    )
+
+
+def gather_weights(w_query, w_key_value, w_out, w_gate, w_up, w_down):
+    if not aligned(w_out):
+        return gather_plain(w_query, w_key_value, w_out, w_gate, w_up, w_down)
+    first = jnp.concatenate([w_query, w_key_value], axis=1)
+    joint, out, gate, up, down = gather_all([first, w_out, w_gate, w_up, w_down])
+    return by_rows(joint), by_columns(out), by_rows(gate), by_rows(up), by_columns(down)
+
+
 def per_device(
     tokens, doc_ids, attn_gain, mlp_gain, w_query, w_key_value, w_out, w_gate, w_up, w_down
 ):
@@ -73,17 +254,12 @@
     pair_width = w_key_value.shape[1]
     head = pair_width // 2
     heads = query_width // head
-    group_query, group_pair = (
-        lax.all_gather(w_query, "fsdp", axis=0, tiled=True),
-        lax.all_gather(w_key_value, "fsdp", axis=0, tiled=True),
-    )
-    pieces = (
-        lax.all_gather(group_query, "dp", axis=0, tiled=True),
-        lax.all_gather(group_pair, "dp", axis=0, tiled=True),
-    )
-    columns = normed
-    query_raw = jnp.dot(columns, pieces[0], preferred_element_type=jnp.float32)
-    pair_raw = jnp.dot(columns, pieces[1], preferred_element_type=jnp.float32)
+    joint, out_full, gate_full, up_full, down_full = gather_weights(
+        w_query, w_key_value, w_out, w_gate, w_up, w_down
+    )
+    raw = jnp.dot(normed, joint, preferred_element_type=jnp.float32)
+    query_raw = raw[:, :query_width]
+    pair_raw = raw[:, query_width:]
     position = rank * rows + jnp.arange(rows, dtype=jnp.int32)
     query = rotate(query_raw.reshape(rows, heads, head), position).astype(jnp.bfloat16)
     keys = rotate(pair_raw[:, None, :head], position)[:, 0, :].astype(jnp.bfloat16)
@@ -109,23 +285,20 @@
     attended = mixed.reshape(rows, query_width).astype(jnp.bfloat16)
     projected = jnp.dot(
         attended,
-        lax.all_gather(w_out, ("dp", "fsdp"), axis=1, tiled=True),
+        out_full,
         preferred_element_type=jnp.float32,
     )
     resid = (tokens.astype(jnp.float32) + projected).astype(jnp.bfloat16)
     resid = lax.optimization_barrier(resid)
     normed_mlp = rms_scale(resid, mlp_gain)
-    pieces = (
-        lax.all_gather(w_gate, ("dp", "fsdp"), axis=0, tiled=True),
-        lax.all_gather(w_up, ("dp", "fsdp"), axis=0, tiled=True),
-    )
+    pieces = (gate_full, up_full)
     columns = normed_mlp
     gate = jnp.dot(columns, pieces[0], preferred_element_type=jnp.float32)
     up_value = jnp.dot(columns, pieces[1], preferred_element_type=jnp.float32)
     hidden = (jax.nn.silu(gate) * up_value).astype(jnp.bfloat16)
     down = jnp.dot(
         hidden,
-        lax.all_gather(w_down, ("dp", "fsdp"), axis=1, tiled=True),
+        down_full,
         preferred_element_type=jnp.float32,
     )
     return (resid.astype(jnp.float32) + down).astype(jnp.bfloat16)

time: 484 us -> 320 us (0.66)
  waiting for transfers between devices: 347 us -> 10.1 us
  Pallas kernels: 0 us -> 189 us
  local copies, waits for them, and re-layouts: 5.75 us -> 35.8 us
  blocking collectives: 16.3 us -> 0 us
  between operations: 13.8 us -> 0.42 us
  matrix products: 55.3 us -> 44.5 us
  starting transfers between devices: 26.3 us -> 17.6 us
    all_gather x6 -> x0, waiting for transfers between devices: 329 us -> none  [the longest x1 81 us: per_device(): lax.all_gather(w_down, ('dp', 'fsdp'), axis=1, tiled=True)]
    pallas_call x0 -> x1, Pallas kernels: none -> 189 us  [gather_all(): pl.pallas_call(functools.partial(gather_kernel, depth, count), out_shape=...]
    reshape x0 -> x3, local copies, waits for them, and re-layouts: none -> 18.8 us  [the longest x2 18.5 us: by_columns(): blocks = full.reshape((-1,) + full.shape[-2:])]
    all_gather x2 -> x0, blocking collectives: 16.3 us -> none  [the longest x1 9.22 us: per_device(): lax.all_gather(w_query, 'fsdp', axis=0, tiled=True)]
    dot_general x4 -> x3, matrix products: 26.3 us -> 15.4 us  [the longest x1 9.56 us: per_device(): down = jnp.dot(hidden, down_full, preferred_element_type=jnp.float32)]
    unnamed x12 -> x38, local copies, waits for them, and re-layouts: 4.78 us -> 15.1 us
    ppermute x6, starting transfers between devices: 26.1 us -> 17.6 us  [shifted(): return lax.ppermute(array, axis, pairs)]
    ppermute x6, waiting for transfers between devices: 16.2 us -> 10.1 us  [shifted(): return lax.ppermute(array, axis, pairs)]
  transfers between devices with their start and end apart: 12 -> 6, of which waited for: 9 -> 1; matrix products, arithmetic and copies ran while one was open for 13% -> 10% of each run, Pallas kernels for 0% -> 60%
where the time goes in v1:
time: 320 us; the launch traced here: 316 us
  Pallas kernels  189 us (59%)
  matrix products  44.5 us (14%)
  local copies, waits for them, and re-layouts  35.8 us (11%)
  other arithmetic  19.1 us (6%)
  starting transfers between devices  17.6 us (6%)
  waiting for transfers between devices  10.1 us (3%)
    pallas_call x1, Pallas kernels, gather_all(): pl.pallas_call(functools.partial(gather_kernel, depth, count), out_shape=...  189 us
    reshape x2, local copies, waits for them, and re-layouts, by_columns(): blocks = full.reshape((-1,) + full.shape[-2:])  18.5 us
    ppermute x6, starting transfers between devices, shifted(): return lax.ppermute(array, axis, pairs)  17.6 us
    unnamed x38, local copies, waits for them, and re-layouts  15.1 us
    dot_general x1, matrix products, weigh_values(): jnp.einsum('hqk,kd->qhd', weights.astype(jnp.bfloat16), values, preferred...  10.6 us
    ppermute x6, waiting for transfers between devices, shifted(): return lax.ppermute(array, axis, pairs)  10.1 us
    reduce_sum x1, other arithmetic, attend_dense(): totals = jnp.sum(weights, axis=2)  9.83 us
    dot_general x1, matrix products, per_device(): down = jnp.dot(hidden, down_full, preferred_element_type=jnp.float32)  9.56 us
  transfers between devices with their start and end apart: 6, of which 1 were waited for; matrix products, arithmetic and copies ran while one was open for 10% of the time, Pallas kernels for 60%

profile of v1, /device:TPU:11, one launch (start us, length us, event | category | flops | bytes accessed | tf_op | source)
XLA Modules:
  0.0 316.0 jit_solution(4346438618545544957)
XLA Ops:
  0.8 3.8 %collective-permute-start.3 = (s32[512]{0:T(512)S(1)}, s32[512]{0:T(512)S(1)}, u32[]{:S(2)}, u32[]{:S(2)}) collective-permute-start(s32[512]{0:T(512)S(1)} %broadcast_add_fusion), channel_id=1, source_target_pairs={{0,1},{1,2},{2,3},{3,4},{4,5},{5,6},{6,7},{7,8},{8,9},{9,10},{10,1... | collective-permute-start | bytes 6152 | tf_op jit(solution)/shard_map/ppermute | solution.py:22
  4.7 3.1 fusion.6
  12.5 188.5 %shard_map.100 = (bf16[4,2,2,2,128,768]{5,4,3,2,1,0:T(8,128)(2,1)S(1)}, bf16[4,2,2,2,512,128]{5,4,3,2,1,0:T(8,128)(2,1)S(1)}, bf16[4,2,2,2,128,1024]{5,4,3,2,1,0...) custom-call(bf16[128,768]{1,0:T(8,128)(2,1)S(1)} %pad_maximum_fusion.2.refs_0_, ...), custom_call_target="tpu_custom_call" | custom-call | tf_op jit(solution)/shard_map/pallas_call | solution.py:186
  201.0 3.2 %copy-done = bf16[4,2,2,2,1024,128]{5,4,3,2,1,0:T(8,128)(2,1)} copy-done((bf16[4,2,2,2,1024,128]{5,4,3,2,1,0:T(8,128)(2,1)}, bf16[4,2,2,2,1024,128]{5,4,3,2,1,0:T(8,128)(2,1)S(1)}, u32[]{:S(2)}) %copy-start) | copy-done | bytes 8388632
  204.3 3.2 %copy-done.6 = bf16[4,2,2,2,128,1024]{5,4,3,2,1,0:T(8,128)(2,1)} copy-done((bf16[4,2,2,2,128,1024]{5,4,3,2,1,0:T(8,128)(2,1)}, bf16[4,2,2,2,128,1024]{5,4,3,2,1,0:T(8,128)(2,1)S(1)}, u32[]{:S(2)}) %copy-start.6) | copy-done | bytes 8388632
  207.5 3.4 %copy-done.7 = bf16[4,2,2,2,128,1024]{5,4,3,2,1,0:T(8,128)(2,1)} copy-done((bf16[4,2,2,2,128,1024]{5,4,3,2,1,0:T(8,128)(2,1)}, bf16[4,2,2,2,128,1024]{5,4,3,2,1,0:T(8,128)(2,1)S(1)}, u32[]{:S(2)}) %copy-start.7) | copy-done | bytes 8388632
  210.9 3.5 %fusion.15 = f32[512,768]{1,0:T(8,128)S(1)} fusion(bf16[4096,768]{1,0:T(8,128)(2,1)S(1)} %bitcast.56, bf16[512,4096]{1,0:T(8,128)(2,1)S(1)} %copy-done.8, f32[4096]{0:T(1024)S(1)} %copy-done.12, f32[512]{0:T(512)S(1)} %add_rsqrt_fusion.1), kind=kOutput, calls=%fused_computation.23 | convolution fusion | flops 3229614080 | bytes 12077056 | tf_op jit(solution)/shard_map/dot_general | solution.py:260
  216.5 3.1 collective-permute-start
  219.6 1.3 slice.46
  222.9 2.3 collective-permute-start.4
  225.5 2.7 collective-permute-start.1
  228.2 1.9 collective-permute-start.5
  230.1 6.5 %copy.27 = bf16[32,512,128]{1,2,0:T(8,128)(2,1)} copy(bf16[32,512,128]{2,1,0:T(8,128)(2,1)} %bitcast.49) | data formatting | bytes 8388608 | tf_op jit(solution)/shard_map/reshape | solution.py:209
  236.7 11.9 %copy.28 = bf16[32,1024,128]{1,2,0:T(8,128)(2,1)} copy(bf16[32,1024,128]{2,1,0:T(8,128)(2,1)} %bitcast.48) | data formatting | bytes 16777216 | tf_op jit(solution)/shard_map/reshape | solution.py:209
  248.7 3.7 %collective-permute-start.2 = (bf16[1024,256]{0,1:T(8,128)(2,1)S(1)}, bf16[1024,256]{0,1:T(8,128)(2,1)S(1)}, u32[]{:S(2)}, u32[]{:S(2)}) collective-permute-start(bf16[1024,256]{0,1:T(8,128)(2,1)S(1)} %pad_maximum_fusion), channel_id=1, source_target_pairs={{0,2},{1,3},{2,4},{3,5},{4,6},{5,7},{6,8},{7,9},{8,10},{9,11},{10,... | collective-permute-start | bytes 1572872 | tf_op jit(solution)/shard_map/ppermute | solution.py:22
  252.4 1.4 fusion.14
  253.9 10.1 %collective-permute-done.2 = bf16[1024,256]{0,1:T(8,128)(2,1)S(1)} collective-permute-done((bf16[1024,256]{0,1:T(8,128)(2,1)S(1)}, bf16[1024,256]{0,1:T(8,128)(2,1)S(1)}, u32[]{:S(2)}, u32[]{:S(2)}) %collective-permute-start.2) | collective-permute-done | bytes 524320 | tf_op jit(solution)/shard_map/ppermute | solution.py:22
  264.1 9.2 %fusion.2 = (f32[4,512]{1,0:T(4,128)S(1)}, f32[2560,512,4]{1,0,2:T(8,128)}) fusion(pred[512,2560]{0,1:T(8,128)(4,1)S(1)} %fusion.14, bf16[512,4,64]{2,0,1:T(8,128)(2,1)S(1)} %get-tuple-element.16, bf16[512,4,64]{2,0,1:T(8,128)(2,1)S(1)} %get-tuple-element.15, bf16[2560,256]{0,1:T(8,128)(2,1)S(1)} %maximum_maximum_fusion), kind=kOutput, calls=%fused_computation.4 | convolution fusion | flops 1358952448 | bytes 23994368 | tf_op jit(solution)/shard_map/qhd,kd->hqk/dot_general | solution.py:46
  273.3 9.8 %fusion = f32[4,512]{1,0:T(4,128)S(1)} fusion(f32[2560,512,4]{1,0,2:T(8,128)} %get-tuple-element.24, f32[4,512]{1,0:T(4,128)S(1)} %get-tuple-element.23, pred[512,2560]{0,1:T(8,128)(4,1)S(1)} %fusion.14), kind=kLoop, calls=%fused_computation.2 | loop fusion | flops 20969472 | bytes 22298624 | tf_op jit(solution)/shard_map/reduce_sum | solution.py:65
  283.1 10.6 %divide_convert_fusion = bf16[512,4,128]{0,2,1:T(8,128)(2,1)S(1)} fusion(f32[2560,512,4]{1,0,2:T(8,128)} %get-tuple-element.24, f32[4,512]{1,0:T(4,128)S(1)} %get-tuple-element.23, pred[512,2560]{0,1:T(8,128)(4,1)S(1)} %fusion.14, bf16[2560,256]{0,1:T(8,128)(2,1)S(1)} %maximum_maximum_fusion, f32[512,4]{0,1:T(4,128)S(1)} %bitcast.60), kind=kOutput, calls=%fused_computation.30 | convolution fusion | flops 1363673088 | bytes 23478272 | tf_op jit(solution)/shard_map/hqk,kd->qhd/dot_general | solution.py:52
  293.7 2.4 fusion.9
  297.1 4.6 %fusion.23 = f32[512,1024]{1,0:T(8,128)S(1)} fusion(bf16[4096,1024]{1,0:T(8,128)(2,1)S(1)} %bitcast.55, bf16[512,4096]{1,0:T(8,128)(2,1)S(1)} %fusion.9, f32[4096]{0:T(1024)S(1)} %copy-done.13, f32[512]{0:T(512)S(1)} %add_rsqrt_fusion), kind=kOutput, calls=%fused_computation.29 | convolution fusion | flops 4303355904 | bytes 14698496 | tf_op jit(solution)/shard_map/dot_general | solution.py:296
  301.7 4.7 %multiply_convert_fusion = bf16[512,1024]{1,0:T(8,128)(2,1)S(1)} fusion(f32[512,1024]{1,0:T(8,128)S(1)} %fusion.23, bf16[4096,1024]{1,0:T(8,128)(2,1)S(1)} %bitcast.52, bf16[512,4096]{1,0:T(8,128)(2,1)S(1)} %fusion.9, f32[4096]{0:T(1024)S(1)} %copy-done.13, f32[512]{0:T(512)S(1)} %add_rsqrt_fusion), kind=kOutput, calls=%fused_computation.26 | convolution fusion | flops 4306501632 | bytes 15747072 | tf_op jit(solution)/shard_map/dot_general | solution.py:297
  306.5 9.6 %fusion.13 = bf16[512,4096]{1,0:T(8,128)(2,1)} fusion(bf16[512,4096]{1,0:T(8,128)(2,1)S(1)} %fusion.9, bf16[512,1024]{1,0:T(8,128)(2,1)S(1)} %multiply_convert_fusion, bf16[1024,4096]{0,1:T(8,128)(2,1)} %bitcast.57), kind=kOutput, calls=%fused_computation.20 | convolution fusion | flops 4301258752 | bytes 17825792 | tf_op jit(solution)/shard_map/dot_general | solution.py:299
  (63 shorter events, 11.0 us)
Async XLA Ops:
  0.0 210.9 %copy-start.8 = (bf16[512,4096]{1,0:T(8,128)(2,1)S(1)}, bf16[512,4096]{1,0:T(8,128)(2,1)}, u32[]{:S(2)}) copy-start(bf16[512,4096]{1,0:T(8,128)(2,1)} %param.10) | copy-start | bytes 12582916
  0.0 210.9 %copy-start.12 = (f32[4096]{0:T(1024)S(1)}, f32[4096]{0:T(1024)}, u32[]{:S(2)}) copy-start(f32[4096]{0:T(1024)} %param.12) | copy-start | bytes 49156
  0.8 222.0 %collective-permute-start.3 = (s32[512]{0:T(512)S(1)}, s32[512]{0:T(512)S(1)}, u32[]{:S(2)}, u32[]{:S(2)}) collective-permute-start(s32[512]{0:T(512)S(1)} %broadcast_add_fusion), channel_id=1, source_target_pairs={{0,1},{1,2},{2,3},{3,4},{4,5},{5,6},{6,7},{7,8},{8,9},{9,10},{10,1... | collective-permute-start | bytes 6152 | tf_op jit(solution)/shard_map/ppermute | solution.py:22
  8.7 1.0 copy-start.2
  9.7 0.9 copy-start.3
  10.6 0.9 copy-start.4
  11.6 0.9 copy-start.5
  201.0 3.3 %copy-start = (bf16[4,2,2,2,1024,128]{5,4,3,2,1,0:T(8,128)(2,1)}, bf16[4,2,2,2,1024,128]{5,4,3,2,1,0:T(8,128)(2,1)S(1)}, u32[]{:S(2)}) copy-start(bf16[4,2,2,2,1024,128]{5,4,3,2,1,0:T(8,128)(2,1)S(1)} %get-tuple-element.14) | copy-start | bytes 25165828
  204.3 3.2 %copy-start.6 = (bf16[4,2,2,2,128,1024]{5,4,3,2,1,0:T(8,128)(2,1)}, bf16[4,2,2,2,128,1024]{5,4,3,2,1,0:T(8,128)(2,1)S(1)}, u32[]{:S(2)}) copy-start(bf16[4,2,2,2,128,1024]{5,4,3,2,1,0:T(8,128)(2,1)S(1)} %get-tuple-element.13) | copy-start | bytes 25165828
  207.5 3.4 %copy-start.7 = (bf16[4,2,2,2,128,1024]{5,4,3,2,1,0:T(8,128)(2,1)}, bf16[4,2,2,2,128,1024]{5,4,3,2,1,0:T(8,128)(2,1)S(1)}, u32[]{:S(2)}) copy-start(bf16[4,2,2,2,128,1024]{5,4,3,2,1,0:T(8,128)(2,1)S(1)} %get-tuple-element.12) | copy-start | bytes 25165828
  210.9 3.5 %copy-start.1 = (bf16[4,2,2,2,512,128]{5,4,3,2,1,0:T(8,128)(2,1)}, bf16[4,2,2,2,512,128]{5,4,3,2,1,0:T(8,128)(2,1)S(1)}, u32[]{:S(2)}) copy-start(bf16[4,2,2,2,512,128]{5,4,3,2,1,0:T(8,128)(2,1)S(1)} %get-tuple-element.11) | copy-start | bytes 12582916
  214.4 1.2 copy-start.11
  216.5 9.0 %collective-permute-start = (bf16[512,256]{0,1:T(8,128)(2,1)S(1)}, bf16[512,256]{0,1:T(8,128)(2,1)S(1)}, u32[]{:S(2)}, u32[]{:S(2)}) collective-permute-start(bf16[512,256]{0,1:T(8,128)(2,1)S(1)} %pad_maximum_fusion.1), channel_id=1, source_target_pairs={{0,1},{1,2},{2,3},{3,4},{4,5},{5,6},{6,7},{7,8},{8,9},{9,10},{10,1... | collective-permute-start | bytes 786440 | tf_op jit(solution)/shard_map/ppermute | solution.py:22
  222.9 5.3 %collective-permute-start.4 = (s32[512]{0:T(512)S(1)}, s32[512]{0:T(512)S(1)}, u32[]{:S(2)}, u32[]{:S(2)}) collective-permute-start(s32[512]{0:T(512)S(1)} %collective-permute-done.3), channel_id=1, source_target_pairs={{0,1},{1,2},{2,3},{3,4},{4,5},{5,6},{6,7},{7,8},{8,9},{9,10},{10,1... | collective-permute-start | bytes 6152 | tf_op jit(solution)/shard_map/ppermute | solution.py:22
  225.5 23.2 %collective-permute-start.1 = (bf16[512,256]{0,1:T(8,128)(2,1)S(1)}, bf16[512,256]{0,1:T(8,128)(2,1)S(1)}, u32[]{:S(2)}, u32[]{:S(2)}) collective-permute-start(bf16[512,256]{0,1:T(8,128)(2,1)S(1)} %collective-permute-done), channel_id=1, source_target_pairs={{0,1},{1,2},{2,3},{3,4},{4,5},{5,6},{6,7},{7,8},{8,9},{9,10},{10,1... | collective-permute-start | bytes 786440 | tf_op jit(solution)/shard_map/ppermute | solution.py:22
  228.2 20.4 %collective-permute-start.5 = (s32[1024]{0:T(1024)S(1)}, s32[1024]{0:T(1024)S(1)}, u32[]{:S(2)}, u32[]{:S(2)}) collective-permute-start(s32[1024]{0:T(1024)S(1)} %pad_add_fusion.1), channel_id=1, source_target_pairs={{0,2},{1,3},{2,4},{3,5},{4,6},{5,7},{6,8},{7,9},{8,10},{9,11},{10,... | collective-permute-start | bytes 12296 | tf_op jit(solution)/shard_map/ppermute | solution.py:22
  248.7 15.3 %collective-permute-start.2 = (bf16[1024,256]{0,1:T(8,128)(2,1)S(1)}, bf16[1024,256]{0,1:T(8,128)(2,1)S(1)}, u32[]{:S(2)}, u32[]{:S(2)}) collective-permute-start(bf16[1024,256]{0,1:T(8,128)(2,1)S(1)} %pad_maximum_fusion), channel_id=1, source_target_pairs={{0,2},{1,3},{2,4},{3,5},{4,6},{5,7},{6,8},{7,9},{8,10},{9,11},{10,... | collective-permute-start | bytes 1572872 | tf_op jit(solution)/shard_map/ppermute | solution.py:22
  273.3 23.8 %slice-start.2 = ((s8[8388608]{0:T(1024)(128)(4,1)}), s8[4194304]{0:T(1024)(128)(4,1)S(1)}, s32[]{:S(2)}) async-start(s8[8388608]{0:T(1024)(128)(4,1)} %bitcast.53), calls=%async_computation.2 | async-start | bytes 8388608
  283.1 10.6 %copy-start.9 = (bf16[512,4096]{1,0:T(8,128)(2,1)S(1)}, bf16[512,4096]{1,0:T(8,128)(2,1)}, u32[]{:S(2)}) copy-start(bf16[512,4096]{1,0:T(8,128)(2,1)} %param.10) | copy-start | bytes 12582916
  283.1 10.6 %copy-start.10 = (bf16[32,512,128]{1,2,0:T(8,128)(2,1)S(1)}, bf16[32,512,128]{1,2,0:T(8,128)(2,1)}, u32[]{:S(2)}) copy-start(bf16[32,512,128]{1,2,0:T(8,128)(2,1)} %copy.27) | copy-start | bytes 12582916
  283.1 13.9 %slice-start.3 = ((s8[8388608]{0:T(1024)(128)(4,1)}), s8[4194304]{0:T(1024)(128)(4,1)S(1)}, s32[]{:S(2)}) async-start(s8[8388608]{0:T(1024)(128)(4,1)} %bitcast.53), calls=%async_computation.3 | async-start | bytes 8388608
  293.7 3.4 %copy-start.13 = (f32[4096]{0:T(1024)S(1)}, f32[4096]{0:T(1024)}, u32[]{:S(2)}) copy-start(f32[4096]{0:T(1024)} %param.13) | copy-start | bytes 49156
  296.1 5.6 %slice-start = ((s8[8388608]{0:T(1024)(128)(4,1)}), s8[4194304]{0:T(1024)(128)(4,1)S(1)}, s32[]{:S(2)}) async-start(s8[8388608]{0:T(1024)(128)(4,1)} %bitcast.50), calls=%async_computation | async-start | bytes 8388608
  297.1 4.6 %slice-start.1 = ((s8[8388608]{0:T(1024)(128)(4,1)}), s8[4194304]{0:T(1024)(128)(4,1)S(1)}, s32[]{:S(2)}) async-start(s8[8388608]{0:T(1024)(128)(4,1)} %bitcast.50), calls=%async_computation.1 | async-start | bytes 8388608

commit v2 on v1

--- a/solution.py
+++ b/solution.py
@@ -165,49 +165,238 @@
     pl.semaphore_wait(barrier, len(peers))
 
 
-def gather_kernel(depth, count, *refs):
-    owns, fulls = refs[:count], refs[count : 2 * count]
-    send, recv, local = refs[2 * count :]
-    spot = (lax.axis_index("dp"), lax.axis_index("fsdp"), depth)
-    rides = [Gather(spot, owns[i], fulls[i], send, recv, local, i) for i in range(count)]
-    greet(rides[0].peers())
-    for ride in rides:
+def normalize(source, gain_ref, target):
+    step = 32
+
+    @pl.loop(0, source.shape[0] // step)
+    def _(index):
+        part = pl.ds(pl.multiple_of(index * step, step), step)
+        target[part, :] = rms_scale(source[part, :], gain_ref[...])
+
+
+def tile_of(full, index, width):
+    columns = pl.ds(pl.multiple_of(index * width, width), width)
+    block = full[:, :, :, :, :, columns]
+    return block.reshape(-1, width)
+
+
+def pair_of(full, index):
+    z, y, x = index // 4, lax.rem(index // 2, 2), lax.rem(index, 2)
+    return jnp.concatenate([full[z, y, x, 0], full[z, y, x, 1]], axis=-1)
+
+
+def turned(values, cosine, sine):
+    half = values.shape[-1] // 2
+    swapped = jnp.concatenate([values[:, half:], values[:, :half]], axis=-1)
+    return (values * cosine + swapped * sine).astype(jnp.bfloat16)
+
+
+def layer_kernel(depth, count, *refs):
+    tokens, attn_gain, mlp_gain, cosine, sine, marks, mark_column = refs[:7]
+    owns = refs[7 : 7 + count]
+    out = refs[7 + count]
+    rest = refs[8 + count :]
+    fulls = rest[:count]
+    (normed, raw, query, pairs, key_marks, attended, gates, hidden) = rest[count : count + 8]
+    send, recv, local, halo_send, halo_recv = rest[count + 8 :]
+    rows = tokens.shape[0]
+    head = pairs.shape[-1] // 2
+    heads = query.shape[-1] // head
+    dp, fsdp = lax.axis_index("dp"), lax.axis_index("fsdp")
+    lanes = 4
+    rank = dp * lanes + fsdp
+    total = depth * 2 * lanes
+
+    def at(offset):
+        there = lax.rem(rank + offset + total, total)
+        return (there // lanes, lax.rem(there, lanes))
+
+    spot = (dp, fsdp, depth)
+    r = [Gather(spot, owns[i], fulls[i], send, recv, local, i) for i in range(count)]
+    offsets = [sign * step for step in range(1, SPAN + 1) for sign in (1, -1)]
+    greet(r[0].peers() + [at(offset) for offset in offsets])
+
+    def halo(kind, step):
+        source = (pairs.at[SPAN], marks)[kind]
+        target = (pairs, key_marks)[kind].at[SPAN - step]
+        return pltpu.make_async_remote_copy(
+            src_ref=source,
+            dst_ref=target,
+            send_sem=halo_send.at[kind, step - 1],
+            recv_sem=halo_recv.at[kind, step - 1],
+            device_id=at(step),
+            device_id_type=MESH,
+        )
+
+    for ride in r:
         ride.s0()
-    for slot in range(count + 3):
-        for stage, lag in (("s1", 0), ("s2", 1), ("s3", 2), ("s4", 3)):
-            if 0 <= slot - lag < count:
-                getattr(rides[slot - lag], stage)()
-
-
-def gather_all(arrays):
+    for step in range(1, SPAN + 1):
+        halo(1, step).start()
+    normalize(tokens, attn_gain, normed)
+    r[0].s1()
+    r[1].s1()
+    r[0].s2()
+    r[2].s1()
+    r[1].s2()
+    r[0].s3()
+    r[0].s4()
+
+    wide = 256
+
+    @pl.loop(0, raw.shape[1] // wide)
+    def _(index):
+        columns = pl.ds(pl.multiple_of(index * wide, wide), wide)
+        raw[:, columns] = jnp.dot(
+            normed[...], tile_of(fulls[0], index, wide), preferred_element_type=jnp.float32
+        )
+
+    base = heads * head
+    pairs[SPAN, :, :head] = turned(raw[:, base : base + head], cosine[...], sine[...])
+    pairs[SPAN, :, head:] = raw[:, base + head :].astype(jnp.bfloat16)
+    for index in range(heads):
+        cut = slice(index * head, (index + 1) * head)
+        query[:, cut] = turned(raw[:, cut], cosine[...], sine[...])
+    for step in range(1, SPAN + 1):
+        halo(0, step).start()
+    r[1].s3()
+    r[3].s1()
+    for step in range(1, SPAN + 1):
+        halo(1, step).wait()
+        halo(0, step).wait()
+
+    part = 256
+    scale = 1.0 / math.sqrt(head)
+    reach = (SPAN + 1) * rows
+
+    @pl.loop(0, (rows // part) * heads)
+    def _(index):
+        chunk, which = index // heads, lax.rem(index, heads)
+        first = pl.multiple_of(chunk * part, part)
+        here = pl.ds(first, part)
+        columns = pl.ds(pl.multiple_of(which * head, head), head)
+        keys = pairs[:, :, :head].reshape(reach, head)
+        values = pairs[:, :, head:].reshape(reach, head)
+        scores = lax.dot_general(
+            query[here, columns], keys, (((1,), (1,)), ((), ())),
+            preferred_element_type=jnp.float32,
+        ) * scale
+        seen = jnp.concatenate([key_marks[step] for step in range(SPAN)] + [marks[...]], axis=-1)
+        key_index = lax.broadcasted_iota(jnp.int32, (1, reach), 1)
+        query_index = lax.broadcasted_iota(jnp.int32, (part, 1), 0) + (first + SPAN * rows)
+        inside = key_index >= (SPAN - rank) * rows
+        seen = jnp.where(inside, seen, -1)
+        allowed = (seen == mark_column[here, :]) & (key_index <= query_index)
+        scores = jnp.where(allowed, scores, NEGATIVE)
+        peak = jnp.max(scores, axis=1, keepdims=True)
+        weights = jnp.exp(scores - peak)
+        sums = jnp.sum(weights, axis=1, keepdims=True)
+        mixed = jnp.dot(weights.astype(jnp.bfloat16), values, preferred_element_type=jnp.float32)
+        attended[here, columns] = (mixed / sums).astype(jnp.bfloat16)
+
+    r[2].s2()
+    r[1].s4()
+    pair_width = 2 * owns[1].shape[1]
+
+    @pl.loop(0, out.shape[1] // pair_width)
+    def _(index):
+        columns = pl.ds(pl.multiple_of(index * pair_width, pair_width), pair_width)
+        moved = jnp.dot(attended[...], pair_of(fulls[1], index), preferred_element_type=jnp.float32)
+        out[:, columns] = (tokens[:, columns].astype(jnp.float32) + moved).astype(jnp.bfloat16)
+
+    r[4].s1()
+    normalize(out, mlp_gain, normed)
+    r[3].s2()
+    r[2].s3()
+    r[2].s4()
+
+    @pl.loop(0, gates.shape[1] // wide)
+    def _(index):
+        columns = pl.ds(pl.multiple_of(index * wide, wide), wide)
+        gates[:, columns] = jnp.dot(
+            normed[...], tile_of(fulls[2], index, wide), preferred_element_type=jnp.float32
+        )
+
+    r[4].s2()
+    r[3].s3()
+    r[3].s4()
+
+    @pl.loop(0, gates.shape[1] // wide)
+    def _(index):
+        columns = pl.ds(pl.multiple_of(index * wide, wide), wide)
+        up = jnp.dot(
+            normed[...], tile_of(fulls[3], index, wide), preferred_element_type=jnp.float32
+        )
+        gate = gates[:, columns]
+        hidden[:, columns] = (gate / (1.0 + jnp.exp(-gate)) * up).astype(jnp.bfloat16)
+
+    r[4].s3()
+    r[4].s4()
+
+    @pl.loop(0, out.shape[1] // pair_width)
+    def _(index):
+        columns = pl.ds(pl.multiple_of(index * pair_width, pair_width), pair_width)
+        moved = jnp.dot(hidden[...], pair_of(fulls[4], index), preferred_element_type=jnp.float32)
+        out[:, columns] = (out[:, columns].astype(jnp.float32) + moved).astype(jnp.bfloat16)
+
+
+def whole_layer(
+    tokens, doc_ids, attn_gain, mlp_gain, w_query, w_key_value, w_out, w_gate, w_up, w_down
+):
     depth = lax.axis_size("dp") // 2
+    rows, model = tokens.shape
+    query_width = w_query.shape[1]
+    pair_width = w_key_value.shape[1]
+    head = pair_width // 2
+    rank = lax.axis_index(("dp", "fsdp"))
+    position = rank * rows + jnp.arange(rows, dtype=jnp.int32)
+    freqs = THETA ** (-2.0 * jnp.arange(head // 2, dtype=jnp.float32) / head)
+    angle = position.astype(jnp.float32)[:, None] * freqs[None, :]
+    cosine = jnp.cos(angle)
+    sine = jnp.sin(angle)
+    cosine = jnp.concatenate([cosine, cosine], axis=1)
+    sine = jnp.concatenate([-sine, sine], axis=1)
+    arrays = [jnp.concatenate([w_query, w_key_value], axis=1), w_out, w_gate, w_up, w_down]
     count = len(arrays)
     copies = depth - 1 + 8
+    marks = doc_ids + 1
+    vmem = pl.BlockSpec(memory_space=pltpu.VMEM)
+    low = jnp.bfloat16
     return pl.pallas_call(
-        functools.partial(gather_kernel, depth, count),
-        out_shape=[
-            jax.ShapeDtypeStruct((depth, 2, 2, 2) + array.shape, array.dtype) for array in arrays
-        ],
-        in_specs=[pl.BlockSpec(memory_space=pl.ANY)] * count,
-        out_specs=[pl.BlockSpec(memory_space=pl.ANY)] * count,
+        functools.partial(layer_kernel, depth, count),
+        out_shape=jax.ShapeDtypeStruct((rows, model), low),
+        in_specs=[vmem] * 7 + [pl.BlockSpec(memory_space=pl.ANY)] * count,
+        out_specs=vmem,
         scratch_shapes=[
+            pltpu.VMEM((depth, 2, 2, 2) + array.shape, array.dtype) for array in arrays
+        ]
+        + [
+            pltpu.VMEM((rows, model), low),
+            pltpu.VMEM((rows, query_width + pair_width), jnp.float32),
+            pltpu.VMEM((rows, query_width), low),
+            pltpu.VMEM((SPAN + 1, rows, pair_width), low),
+            pltpu.VMEM((SPAN, 1, rows), jnp.int32),
+            pltpu.VMEM((rows, query_width), low),
+            pltpu.VMEM((rows, w_gate.shape[1]), jnp.float32),
+            pltpu.VMEM((rows, w_gate.shape[1]), low),
             pltpu.SemaphoreType.DMA((count, copies)),
             pltpu.SemaphoreType.DMA((count, copies)),
             pltpu.SemaphoreType.DMA((count,)),
+            pltpu.SemaphoreType.DMA((2, SPAN)),
+            pltpu.SemaphoreType.DMA((2, SPAN)),
         ],
         compiler_params=pltpu.CompilerParams(
-            collective_id=0, has_side_effects=True, vmem_limit_bytes=4 << 20
+            collective_id=0, has_side_effects=True, vmem_limit_bytes=67043328
         ),
-    )(*arrays)
-
-
-def by_rows(full):
-    return full.reshape(-1, full.shape[-1])
-
-
-def by_columns(full):
-    blocks = full.reshape((-1,) + full.shape[-2:])
-    return jnp.transpose(blocks, (1, 0, 2)).reshape(blocks.shape[1], -1)
+    )(
+        tokens,
+        attn_gain[None, :],
+        mlp_gain[None, :],
+        cosine,
+        sine,
+        marks[None, :],
+        marks[:, None],
+        *arrays,
+    )
 
 
 def gather_plain(w_query, w_key_value, w_out, w_gate, w_up, w_down):
@@ -236,17 +425,13 @@
     )
 
 
-def gather_weights(w_query, w_key_value, w_out, w_gate, w_up, w_down):
-    if not aligned(w_out):
-        return gather_plain(w_query, w_key_value, w_out, w_gate, w_up, w_down)
-    first = jnp.concatenate([w_query, w_key_value], axis=1)
-    joint, out, gate, up, down = gather_all([first, w_out, w_gate, w_up, w_down])
-    return by_rows(joint), by_columns(out), by_rows(gate), by_rows(up), by_columns(down)
-
-
 def per_device(
     tokens, doc_ids, attn_gain, mlp_gain, w_query, w_key_value, w_out, w_gate, w_up, w_down
 ):
+    if aligned(w_out):
+        return whole_layer(
+            tokens, doc_ids, attn_gain, mlp_gain, w_query, w_key_value, w_out, w_gate, w_up, w_down
+        )
     rows = tokens.shape[0]
     rank = lax.axis_index(("dp", "fsdp"))
     normed = rms_scale(tokens, attn_gain)
@@ -254,7 +439,7 @@
     pair_width = w_key_value.shape[1]
     head = pair_width // 2
     heads = query_width // head
-    joint, out_full, gate_full, up_full, down_full = gather_weights(
+    joint, out_full, gate_full, up_full, down_full = gather_plain(
         w_query, w_key_value, w_out, w_gate, w_up, w_down
     )
     raw = jnp.dot(normed, joint, preferred_element_type=jnp.float32)

time: 320 us -> 232 us (0.72); the launches traced: 316 us -> 231 us
  matrix products: 44.5 us -> 0 us
  Pallas kernels: 189 us -> 222 us
  local copies, waits for them, and re-layouts: 35.8 us -> 5.57 us
  starting transfers between devices: 17.6 us -> 0 us
  other arithmetic: 19.1 us -> 4.31 us
  waiting for transfers between devices: 10.1 us -> 0 us
    dot_general x7 -> x0, matrix products: 44.5 us -> none  [the longest x1 10.6 us: weigh_values(): jnp.einsum('hqk,kd->qhd', weights.astype(jnp.bfloat16), values, preferred...]
    pallas_call x1, Pallas kernels: 189 us -> 222 us  [whole_layer(): pl.pallas_call(functools.partial(layer_kernel, depth, count), out_shape=j...]
    reshape x3 -> x0, local copies, waits for them, and re-layouts: 18.8 us -> none  [the longest x2 18.5 us: by_columns(): blocks = full.reshape((-1,) + full.shape[-2:])]
    ppermute x6 -> x0, starting transfers between devices: 17.6 us -> none  [shifted(): return lax.ppermute(array, axis, pairs)]
    reduce_sum x3 -> x0, other arithmetic: 13.8 us -> none  [the longest x1 9.83 us: attend_dense(): totals = jnp.sum(weights, axis=2)]
    unnamed x38 -> x3, local copies, waits for them, and re-layouts: 15.1 us -> 4.7 us
    ppermute x6 -> x0, waiting for transfers between devices: 10.1 us -> none  [shifted(): return lax.ppermute(array, axis, pairs)]
  transfers between devices with their start and end apart: 6 -> 0, of which waited for: 1 -> 0; matrix products, arithmetic and copies ran while one was open for 10% -> 0% of each run, Pallas kernels for 60% -> 0%
where the time goes in v2:
time: 232 us; the launch traced here: 231 us
  Pallas kernels  222 us (96%)
  local copies, waits for them, and re-layouts  5.57 us (2%)
  other arithmetic  4.31 us (2%)
    pallas_call x1, Pallas kernels, whole_layer(): pl.pallas_call(functools.partial(layer_kernel, depth, count), out_shape=j...  222 us
    unnamed x3, local copies, waits for them, and re-layouts  4.7 us

profile of v2, /device:TPU:11, one launch (start us, length us, event | category | flops | bytes accessed | tf_op | source)
XLA Modules:
  0.0 231.4 jit_solution(9737738519457119692)
XLA Ops:
  0.0 0.7 broadcast_add_fusion
  0.7 0.0 copy-start
  0.7 1.6 pad_maximum_fusion.2.refs_7_
  2.3 0.9 copy.11.refs_6_
  3.2 1.0 fusion
  4.2 1.0 pad_maximum_fusion
  5.2 0.0 copy-done
  5.2 221.5 %shard_map.100 = bf16[512,4096]{1,0:T(8,128)(2,1)} custom-call(bf16[512,4096]{1,0:T(8,128)(2,1)} %refs_0_.1, f32[1,4096]{1,0:T(1,128)} %bitcast.6, f32[1,4096]{1,0:T(1,128)} %bitcast.7, f32[512,128]{1,0:T(8,128)} %get-tuple-element.8.refs_3_, f32[512,128]{1,0:T(8,128)} %get-tuple-element.9.refs_4_, s32[1,512]{1,0:T(1,128)} %bitcast.5, ...), custom_call_target="tpu_custom_call" | custom-call | tf_op jit(solution)/shard_map/pallas_call | solution.py:364
  226.7 4.7 %copy.13 = bf16[512,4096]{1,0:T(8,128)(2,1)} copy(bf16[512,4096]{1,0:T(8,128)(2,1)} %shard_map.100) | data formatting | bytes 8388608
  (2 shorter events, 0.0 us)
Async XLA Ops:
  0.7 4.5 %copy-start = (s32[512]{0:T(512)}, s32[512]{0:T(512)S(1)}, u32[]{:S(2)}) copy-start(s32[512]{0:T(512)S(1)} %broadcast_add_fusion) | copy-start | bytes 6148

commit v3 on v2

--- a/solution.py
+++ b/solution.py
@@ -228,15 +228,17 @@
             device_id_type=MESH,
         )
 
-    for ride in r:
-        ride.s0()
+    r[0].s0()
     for step in range(1, SPAN + 1):
         halo(1, step).start()
     normalize(tokens, attn_gain, normed)
     r[0].s1()
+    r[1].s0()
     r[1].s1()
+    r[2].s0()
     r[0].s2()
     r[2].s1()
+    r[3].s0()
     r[1].s2()
     r[0].s3()
     r[0].s4()
@@ -260,6 +262,7 @@
         halo(0, step).start()
     r[1].s3()
     r[3].s1()
+    r[4].s0()
     for step in range(1, SPAN + 1):
         halo(1, step).wait()
         halo(0, step).wait()

time: 232 us -> 213 us (0.918)
  Pallas kernels: 222 us -> 202 us
    pallas_call x1, Pallas kernels: 222 us -> 202 us  [whole_layer(): pl.pallas_call(functools.partial(layer_kernel, depth, count), out_shape=j...]
where the time goes in v3:
time: 213 us; the launch traced here: 212 us
  Pallas kernels  202 us (95%)
  local copies, waits for them, and re-layouts  5.57 us (3%)
  other arithmetic  4.31 us (2%)
    pallas_call x1, Pallas kernels, whole_layer(): pl.pallas_call(functools.partial(layer_kernel, depth, count), out_shape=j...  202 us
    unnamed x3, local copies, waits for them, and re-layouts  4.7 us

profile of v3, /device:TPU:11, one launch (start us, length us, event | category | flops | bytes accessed | tf_op | source)
XLA Modules:
  0.0 211.7 jit_solution(10358085370026891847)
XLA Ops:
  0.0 0.7 broadcast_add_fusion
  0.7 0.0 copy-start
  0.7 1.6 pad_maximum_fusion.2.refs_7_
  2.3 0.9 copy.11.refs_6_
  3.2 1.0 fusion
  4.2 1.0 pad_maximum_fusion
  5.2 0.0 copy-done
  5.2 201.8 %shard_map.100 = bf16[512,4096]{1,0:T(8,128)(2,1)} custom-call(bf16[512,4096]{1,0:T(8,128)(2,1)} %refs_0_.1, f32[1,4096]{1,0:T(1,128)} %bitcast.6, f32[1,4096]{1,0:T(1,128)} %bitcast.7, f32[512,128]{1,0:T(8,128)} %get-tuple-element.8.refs_3_, f32[512,128]{1,0:T(8,128)} %get-tuple-element.9.refs_4_, s32[1,512]{1,0:T(1,128)} %bitcast.5, ...), custom_call_target="tpu_custom_call" | custom-call | tf_op jit(solution)/shard_map/pallas_call | solution.py:367
  207.0 4.7 %copy.13 = bf16[512,4096]{1,0:T(8,128)(2,1)} copy(bf16[512,4096]{1,0:T(8,128)(2,1)} %shard_map.100) | data formatting | bytes 8388608
  (2 shorter events, 0.0 us)
Async XLA Ops:
  0.7 4.5 %copy-start = (s32[512]{0:T(512)}, s32[512]{0:T(512)S(1)}, u32[]{:S(2)}) copy-start(s32[512]{0:T(512)S(1)} %broadcast_add_fusion) | copy-start | bytes 6148
